TPU v7x, 32 devices: a whole 2x2x4 slice. The times are simulated.
32 devices in a mesh: dp: 16 (over z, x, core), rows: 2 (over y).
Axes of the slice: x: 2, y: 2, z: 4, core: 2. Of those that a mesh axis runs over, the one named last changes fastest.
Arguments:
- fine_level: bfloat16 [16, 32, 64, 256], P('dp', 'rows'), may hold values from -6 to 6
- out_grad: bfloat16 [16, 32, 64, 256], P('dp', 'rows'), may hold values from -6 to 6
- fine_input: bfloat16 [16, 32, 64, 256], P('dp', 'rows'), may hold values from -6 to 6
- mid_input: bfloat16 [16, 16, 32, 512], P('dp', None, None, 'rows'), may hold values from -6 to 6
- top_input: bfloat16 [16, 8, 16, 1024], P('dp', None, None, 'rows'), may hold values from -6 to 6
- smooth_weight: bfloat16 [3, 3, 256, 256], replicated, may hold values from -0.125 to 0.125
- fine_lateral: bfloat16 [256, 256], replicated, may hold values from -0.375 to 0.375
- mid_lateral: bfloat16 [512, 256], P('rows'), may hold values from -0.375 to 0.375
- top_lateral: bfloat16 [1024, 256], P('rows'), may hold values from -0.375 to 0.375
Outputs:
- grad_fine: bfloat16 [16, 32, 64, 256], P('dp', 'rows')
- grad_mid: bfloat16 [16, 16, 32, 512], P('dp', None, None, 'rows')
- grad_top: bfloat16 [16, 8, 16, 1024], P('dp', None, None, 'rows')
- kernel_grads: float32 [2560, 256], P('dp')
- midlat_grad: float32 [512, 256], P('rows')
- toplat_grad: float32 [1024, 256], P('rows')
All inputs are finite; a program needn't handle non-finite values.
Results may differ from a plain program's by a relative error of at most 0.0062.
Values may be sent and summed in bfloat16 or wider, within the bound.
No kernel may reach another device: no remote copies, remote signals or barrier semaphores. Data moves between devices by JAX's collectives and lax.ppermute only.
A program may use at most 64 MiB of HBM per device.

v0:
```python
import jax
import jax.numpy as jnp
from jax import lax
from jax.sharding import PartitionSpec as P


def with_halo(value, sides, width):
    for axis, dim in sides:
        count, length = (lax.axis_size(axis), value.shape[dim])
        up = [(i, (i + 1) % count) for i in range(count - 1)]
        down = [(j, i) for i, j in up]
        last = lax.slice_in_dim(value, length - width, length, axis=dim)
        leading = lax.slice_in_dim(value, 0, width, axis=dim)
        before = lax.ppermute(last, axis, up)
        after = lax.ppermute(leading, axis, down)
        value = jnp.concatenate([before, value, after], axis=dim)
    return value


def pool_two(field):
    images, rows_n, cols_n, chans = field.shape
    return field.reshape(images, rows_n // 2, 2, cols_n // 2, 2, chans).sum(axis=(2, 4))


def contract_last(left, right):
    return lax.dot_general(
        left, right, (((1,), (1,)), ((), ())), preferred_element_type=jnp.float32
    )


def contract_first(left, right):
    return lax.dot_general(
        left, right, (((0,), (0,)), ((), ())), preferred_element_type=jnp.float32
    )


def body(
    fine_level,
    out_grad,
    fine_input,
    mid_input,
    top_input,
    smooth_weight,
    fine_lateral,
    mid_lateral,
    top_lateral,
):
    images, strip, width, chans = out_grad.shape
    cells = images * strip * width
    rimmed = with_halo(out_grad, (("rows", 1),), 1)
    rimmed = jnp.pad(rimmed, ((0, 0), (0, 0), (1, 1), (0, 0)))
    fine_flat = fine_level.reshape(cells, chans)
    level_grad = jnp.zeros((cells, chans), jnp.float32)
    pieces = []
    for tap_a in range(3):
        for tap_b in range(3):
            shifted = rimmed[
                :, 2 - tap_a : 2 - tap_a + strip, 2 - tap_b : 2 - tap_b + width, :
            ].reshape(cells, chans)
            level_grad = level_grad + contract_last(shifted, smooth_weight[tap_a, tap_b])
            pieces.append(contract_first(fine_flat, shifted))
    fine_grad = level_grad.astype(jnp.bfloat16)
    grad_fine = (
        contract_last(fine_grad, fine_lateral)
        .astype(jnp.bfloat16)
        .reshape(images, strip, width, -1)
    )
    pieces.append(contract_first(fine_input.reshape(cells, -1), fine_grad))
    kernel_term = jnp.concatenate(pieces, axis=0)
    share = lax.psum_scatter(kernel_term, "dp", scatter_dimension=0, tiled=True)
    kernel_grads = lax.psum(share, "rows")
    pooled = pool_two(level_grad.reshape(images, strip, width, chans)).astype(jnp.bfloat16)
    mid_grad = lax.all_gather(pooled, "rows", axis=1, tiled=True)
    top_grad = pool_two(mid_grad.astype(jnp.float32)).astype(jnp.bfloat16)
    mid_flat = mid_grad.reshape(-1, chans)
    top_flat = top_grad.reshape(-1, chans)
    grad_mid = contract_last(mid_flat, mid_lateral).astype(jnp.bfloat16).reshape(mid_input.shape)
    grad_top = contract_last(top_flat, top_lateral).astype(jnp.bfloat16).reshape(top_input.shape)
    mid_term = contract_first(mid_input.reshape(mid_flat.shape[0], -1), mid_flat)
    top_term = contract_first(top_input.reshape(top_flat.shape[0], -1), top_flat)
    midlat_grad, toplat_grad = lax.psum((mid_term, top_term), "dp")
    return (grad_fine, grad_mid, grad_top, kernel_grads, midlat_grad, toplat_grad)


def solution(mesh):
    placed = (
        P("dp", "rows", None, None),
        P("dp", "rows", None, None),
        P("dp", "rows", None, None),
        P("dp", None, None, "rows"),
        P("dp", None, None, "rows"),
        P(),
        P(),
        P("rows", None),
        P("rows", None),
    )
    return jax.shard_map(
        body,
        mesh=mesh,
        in_specs=placed,
        out_specs=(
            P("dp", "rows", None, None),
            P("dp", None, None, "rows"),
            P("dp", None, None, "rows"),
            P("dp", None),
            P("rows", None),
            P("rows", None),
        ),
        check_vma=False,
    )
```

profile of v0, /device:TPU:0, one launch (start us, length us, event | category | flops | bytes accessed | tf_op | source)
XLA Modules:
  0.0 226.8 jit_solution(9523882617823128854)
XLA Ops:
  7.2 0.8 fusion.66
  8.1 4.9 %collective-permute-start = (bf16[1,1,64,256]{3,2,1,0:T(8,128)(2,1)S(1)}, bf16[1,1,64,256]{3,2,1,0:T(8,128)(2,1)S(1)}, u32[]{:S(2)}, u32[]{:S(2)}) collective-permute-start(bf16[1,1,64,256]{3,2,1,0:T(8,128)(2,1)S(1)} %get-tuple-element.28), channel_id=1, source_target_pairs={{0,1},{2,3},{4,5},{6,7},{8,9},{10,11},{12,13},{14,15},{16,17},{18,... | collective-permute-start | bytes 98312 | tf_op jit(solution)/shard_map/ppermute | solution.py:14
  13.0 1.3 collective-permute-start.1
  14.5 4.2 %collective-permute-done.1 = bf16[1,1,64,256]{3,2,1,0:T(8,128)(2,1)S(1)} collective-permute-done((bf16[1,1,64,256]{3,2,1,0:T(8,128)(2,1)S(1)}, bf16[1,1,64,256]{3,2,1,0:T(8,128)(2,1)S(1)}, u32[]{:S(2)}, u32[]{:S(2)}) %collective-permute-start.1) | collective-permute-done | bytes 32800 | tf_op jit(solution)/shard_map/ppermute | solution.py:15
  18.8 1.3 fusion.16
  20.1 0.5 fusion.65
  20.6 1.1 fusion.11
  21.8 1.1 fusion.10
  22.8 1.0 fusion.9
  23.9 1.1 fusion.8
  24.9 1.0 fusion.7
  26.0 1.1 fusion.6
  27.0 1.1 fusion.5
  28.1 1.1 fusion.4
  29.2 1.0 fusion.3
  33.3 0.4 copy-done.3
  33.7 1.1 fusion.2
  34.8 0.6 reshape_reshape.3
  35.4 0.9 reduce_sum.18
  36.3 5.6 %all-gather = bf16[16,32,256]{2,1,0:T(8,128)(2,1)S(1)} all-gather(bf16[8,32,256]{2,1,0:T(8,128)(2,1)S(1)} %reduce_sum.18), channel_id=2, replica_groups=mesh['dp'=16,'rows'=2] {'rows'}, dimensions={0}, use_global_device_ids=true | all-gather | bytes 393216 | tf_op jit(solution)/shard_map/all_gather | solution.py:73
  42.0 0.5 reduce.2
  42.5 1.0 convolution_bitcast_fusion
  43.6 1.0 convolution_bitcast_fusion.1
  44.6 1.0 convolution_convert_fusion.1
  45.6 1.1 convolution_convert_fusion
  46.7 52.6 %reduce-scatter.2.cloned.1.call-done = f32[160,256]{1,0:T(8,128)} async-done(((f32[2560,256]{1,0:T(8,128)}), f32[160,256]{1,0:T(8,128)}) %reduce-scatter.2.cloned.1.call-update) | async-done | bytes 163856 | tf_op jit(solution)/shard_map/reduce_scatter | solution.py:70
  99.4 0.9 convolution_convert_fusion.2
  100.3 95.1 %all-reduce.7.cloned.1.call-done = (f32[256,256]{0,1:T(8,128)}, f32[512,256]{0,1:T(8,128)}) async-done(((f32[256,256]{0,1:T(8,128)}, f32[512,256]{0,1:T(8,128)}), (f32[256,256]{0,1:T(8,128)}, f32[512,256]{0,1:T(8,128)})) %all-reduce.7.cloned.1.call-update) | async-done | bytes 786448 | tf_op jit(solution)/shard_map/psum | solution.py:81
  195.4 1.8 copy.17
  197.1 2.0 copy.18
  199.2 19.5 %all-reduce.5.cloned.1.call-done = f32[160,256]{1,0:T(8,128)} async-done(((f32[160,256]{1,0:T(8,128)}), f32[160,256]{1,0:T(8,128)}) %all-reduce.5.cloned.1.call-update) | async-done | bytes 163856 | tf_op jit(solution)/shard_map/psum | solution.py:71
  218.7 1.6 copy.31
  (35 shorter events, 3.6 us)
Async XLA Ops:
  7.2 13.4 %copy-start = (bf16[1,16,64,256]{3,2,1,0:T(8,128)(2,1)S(1)}, bf16[1,16,64,256]{3,2,1,0:T(8,128)(2,1)}, u32[]{:S(2)}) copy-start(bf16[1,16,64,256]{3,2,1,0:T(8,128)(2,1)} %param.9) | copy-start | bytes 1572868
  7.2 92.2 %reduce-scatter.2.cloned.1.call-start = ((), (), s32[]{:S(2)}) async-start(), calls=%async_computation.1 | async-start | bytes 2785280 | tf_op jit(solution)/shard_map/reduce_scatter | solution.py:70
  8.1 6.5 %collective-permute-start = (bf16[1,1,64,256]{3,2,1,0:T(8,128)(2,1)S(1)}, bf16[1,1,64,256]{3,2,1,0:T(8,128)(2,1)S(1)}, u32[]{:S(2)}, u32[]{:S(2)}) collective-permute-start(bf16[1,1,64,256]{3,2,1,0:T(8,128)(2,1)S(1)} %get-tuple-element.28), channel_id=1, source_target_pairs={{0,1},{2,3},{4,5},{6,7},{8,9},{10,11},{12,13},{14,15},{16,17},{18,... | collective-permute-start | bytes 98312 | tf_op jit(solution)/shard_map/ppermute | solution.py:14
  13.0 5.8 %collective-permute-start.1 = (bf16[1,1,64,256]{3,2,1,0:T(8,128)(2,1)S(1)}, bf16[1,1,64,256]{3,2,1,0:T(8,128)(2,1)S(1)}, u32[]{:S(2)}, u32[]{:S(2)}) collective-permute-start(bf16[1,1,64,256]{3,2,1,0:T(8,128)(2,1)S(1)} %get-tuple-element.29), channel_id=1, source_target_pairs={{1,0},{3,2},{5,4},{7,6},{9,8},{11,10},{13,12},{15,14},{17,16},{19,... | collective-permute-start | bytes 98312 | tf_op jit(solution)/shard_map/ppermute | solution.py:15
  20.0 1.7 copy-start.1
  27.0 3.2 %copy-start.2 = (bf16[3,3,256,256]{3,2,1,0:T(8,128)(2,1)S(1)}, bf16[3,3,256,256]{3,2,1,0:T(8,128)(2,1)}, u32[]{:S(2)}) copy-start(bf16[3,3,256,256]{3,2,1,0:T(8,128)(2,1)} %param.14) | copy-start | bytes 3538948
  32.6 1.0 copy-start.3
  34.7 7.8 %copy-start.8 = (bf16[1,8,16,512]{3,2,1,0:T(8,128)(2,1)S(1)}, bf16[1,8,16,512]{3,2,1,0:T(8,128)(2,1)}, u32[]{:S(2)}) copy-start(bf16[1,8,16,512]{3,2,1,0:T(8,128)(2,1)} %param.13) | copy-start | bytes 393220
  34.7 8.8 %copy-start.7 = (bf16[1,16,32,256]{3,2,1,0:T(8,128)(2,1)S(1)}, bf16[1,16,32,256]{3,2,1,0:T(8,128)(2,1)}, u32[]{:S(2)}) copy-start(bf16[1,16,32,256]{3,2,1,0:T(8,128)(2,1)} %param.12) | copy-start | bytes 786436
  34.8 160.6 %all-reduce.7.cloned.1.call-start = ((), (), s32[]{:S(2)}) async-start(), calls=%async_computation.3 | async-start | bytes 1572864 | tf_op jit(solution)/shard_map/psum | solution.py:81
  41.9 2.7 %copy-start.5 = (bf16[256,256]{1,0:T(8,128)(2,1)S(1)}, bf16[256,256]{1,0:T(8,128)(2,1)}, u32[]{:S(2)}) copy-start(bf16[256,256]{1,0:T(8,128)(2,1)} %param.16) | copy-start | bytes 393220
  42.0 3.5 %copy-start.6 = (bf16[256,256]{1,0:T(8,128)(2,1)S(1)}, bf16[256,256]{1,0:T(8,128)(2,1)}, u32[]{:S(2)}) copy-start(bf16[256,256]{1,0:T(8,128)(2,1)} %param.15) | copy-start | bytes 393220
  43.6 55.8 %copy-start.4 = (bf16[512,256]{1,0:T(8,128)(2,1)S(1)}, bf16[512,256]{1,0:T(8,128)(2,1)}, u32[]{:S(2)}) copy-start(bf16[512,256]{1,0:T(8,128)(2,1)} %param.17) | copy-start | bytes 786436
  44.6 174.2 %all-reduce.5.cloned.1.call-start = ((), (), s32[]{:S(2)}) async-start(), calls=%async_computation.2 | async-start | bytes 327680 | tf_op jit(solution)/shard_map/psum | solution.py:71
Sparse Core Ops, SparseCore 0:
  34.8 64.4 reduce-scatter.1
  103.4 91.8 all-reduce.6
  197.6 21.0 all-reduce.4
where the time goes:
time: 227 us
  waiting for transfers between devices  172 us (76%)
  matrix products  18.6 us (8%)
  between operations  13.9 us (6%)
  local copies, waits for them, and re-layouts  7.89 us (3%)
  starting transfers between devices  6.3 us (3%)
  blocking collectives  5.64 us (2%)
  other arithmetic  2.65 us (1%)
    psum x1, waiting for transfers between devices, body(): midlat_grad, toplat_grad = lax.psum((mid_term, top_term), 'dp')  95.1 us
    reduce_scatter x1, waiting for transfers between devices, body(): share = lax.psum_scatter(kernel_term, 'dp', scatter_dimension=0, tiled=True)  52.6 us
    psum x1, waiting for transfers between devices, body(): kernel_grads = lax.psum(share, 'rows')  19.5 us
    dot_general x12, matrix products, contract_first(): lax.dot_general(left, right, (((0,), (0,)), ((), ())), preferred_element_...  12.6 us
    dot_general x12, matrix products, contract_last(): lax.dot_general(left, right, (((1,), (1,)), ((), ())), preferred_element_...  5.95 us
    unnamed x21, local copies, waits for them, and re-layouts  5.82 us
    all_gather x1, blocking collectives, body(): mid_grad = lax.all_gather(pooled, 'rows', axis=1, tiled=True)  5.64 us
    ppermute x1, starting transfers between devices, with_halo(): before = lax.ppermute(last, axis, up)  4.89 us
  transfers between devices with their start and end apart: 5, of which 5 were waited for; matrix products, arithmetic and copies ran while one was open for 5% of the time, Pallas kernels for 0%

commit v1 on v0

--- a/solution.py
+++ b/solution.py
@@ -68,7 +68,7 @@
     pieces.append(contract_first(fine_input.reshape(cells, -1), fine_grad))
     kernel_term = jnp.concatenate(pieces, axis=0)
     share = lax.psum_scatter(kernel_term, "dp", scatter_dimension=0, tiled=True)
-    kernel_grads = lax.psum(share, "rows")
+    kernel_grads = jnp.sum(lax.all_gather(share, "rows"), axis=0)
     pooled = pool_two(level_grad.reshape(images, strip, width, chans)).astype(jnp.bfloat16)
     mid_grad = lax.all_gather(pooled, "rows", axis=1, tiled=True)
     top_grad = pool_two(mid_grad.astype(jnp.float32)).astype(jnp.bfloat16)

time: 227 us -> 214 us (0.943)
  waiting for transfers between devices: 172 us -> 156 us
  blocking collectives: 5.64 us -> 11.8 us
  matrix products: 18.6 us -> 14 us
    psum x1 -> x0, waiting for transfers between devices: 19.5 us -> none  [body(): kernel_grads = lax.psum(share, 'rows')]
    reduce_scatter x1, waiting for transfers between devices: 52.6 us -> 63.2 us  [body(): share = lax.psum_scatter(kernel_term, 'dp', scatter_dimension=0, tiled=True)]
    psum x1, waiting for transfers between devices: 95.1 us -> 88.2 us  [body(): midlat_grad, toplat_grad = lax.psum((mid_term, top_term), 'dp')]
    all_gather x0 -> x1, blocking collectives: none -> 6.19 us  [body(): kernel_grads = jnp.sum(lax.all_gather(share, 'rows'), axis=0)]
    dot_general x12, matrix products: 12.6 us -> 8.03 us  [contract_first(): lax.dot_general(left, right, (((0,), (0,)), ((), ())), preferred_element_...]
    unnamed x21 -> x20, local copies, waits for them, and re-layouts: 5.82 us -> 5.65 us
  transfers between devices with their start and end apart: 5 -> 4, of which waited for: 5 -> 4; matrix products, arithmetic and copies ran while one was open for 5% -> 4% of each run, Pallas kernels for 0% -> 0%
where the time goes in v1:
time: 214 us; the launch traced here: 213 us
  waiting for transfers between devices  156 us (73%)
  between operations  14.3 us (7%)
  matrix products  14 us (7%)
  blocking collectives  11.8 us (6%)
  local copies, waits for them, and re-layouts  7.72 us (4%)
  starting transfers between devices  6.26 us (3%)
  other arithmetic  3.4 us (2%)
    psum x1, waiting for transfers between devices, body(): midlat_grad, toplat_grad = lax.psum((mid_term, top_term), 'dp')  88.2 us
    reduce_scatter x1, waiting for transfers between devices, body(): share = lax.psum_scatter(kernel_term, 'dp', scatter_dimension=0, tiled=True)  63.2 us
    dot_general x12, matrix products, contract_first(): lax.dot_general(left, right, (((0,), (0,)), ((), ())), preferred_element_...  8.03 us
    all_gather x1, blocking collectives, body(): kernel_grads = jnp.sum(lax.all_gather(share, 'rows'), axis=0)  6.19 us
    dot_general x12, matrix products, contract_last(): lax.dot_general(left, right, (((1,), (1,)), ((), ())), preferred_element_...  5.93 us
    unnamed x20, local copies, waits for them, and re-layouts  5.65 us
    all_gather x1, blocking collectives, body(): mid_grad = lax.all_gather(pooled, 'rows', axis=1, tiled=True)  5.64 us
    ppermute x1, starting transfers between devices, with_halo(): before = lax.ppermute(last, axis, up)  4.89 us
  transfers between devices with their start and end apart: 4, of which 4 were waited for; matrix products, arithmetic and copies ran while one was open for 4% of the time, Pallas kernels for 0%

profile of v1, /device:TPU:0, one launch (start us, length us, event | category | flops | bytes accessed | tf_op | source)
XLA Modules:
  0.0 213.4 jit_solution(14202523876867171814)
XLA Ops:
  7.2 0.8 fusion.66
  8.1 4.9 %collective-permute-start = (bf16[1,1,64,256]{3,2,1,0:T(8,128)(2,1)S(1)}, bf16[1,1,64,256]{3,2,1,0:T(8,128)(2,1)S(1)}, u32[]{:S(2)}, u32[]{:S(2)}) collective-permute-start(bf16[1,1,64,256]{3,2,1,0:T(8,128)(2,1)S(1)} %get-tuple-element.28), channel_id=1, source_target_pairs={{0,1},{2,3},{4,5},{6,7},{8,9},{10,11},{12,13},{14,15},{16,17},{18,... | collective-permute-start | bytes 98312 | tf_op jit(solution)/shard_map/ppermute | solution.py:14
  13.0 1.3 collective-permute-start.1
  14.5 4.2 %collective-permute-done.1 = bf16[1,1,64,256]{3,2,1,0:T(8,128)(2,1)S(1)} collective-permute-done((bf16[1,1,64,256]{3,2,1,0:T(8,128)(2,1)S(1)}, bf16[1,1,64,256]{3,2,1,0:T(8,128)(2,1)S(1)}, u32[]{:S(2)}, u32[]{:S(2)}) %collective-permute-start.1) | collective-permute-done | bytes 32800 | tf_op jit(solution)/shard_map/ppermute | solution.py:15
  18.8 1.3 fusion.16
  20.1 0.5 fusion.65
  20.6 0.4 fusion.11
  21.2 0.4 fusion.10
  21.5 0.3 fusion.9
  21.9 0.4 fusion.8
  22.3 0.3 fusion.7
  22.6 0.3 fusion.6
  23.0 0.4 fusion.5
  24.2 0.4 fusion.4
  24.6 1.5 copy-done.2
  28.4 0.6 reshape_reshape.3
  29.1 0.9 reduce_sum.27
  30.0 5.6 %all-gather = bf16[16,32,256]{2,1,0:T(8,128)(2,1)S(1)} all-gather(bf16[8,32,256]{2,1,0:T(8,128)(2,1)S(1)} %reduce_sum.27), channel_id=2, replica_groups=mesh['dp'=16,'rows'=2] {'rows'}, dimensions={0}, use_global_device_ids=true | all-gather | bytes 393216 | tf_op jit(solution)/shard_map/all_gather | solution.py:73
  35.7 2.0 convolution_bitcast_fusion.1
  37.7 0.5 reduce.2
  38.2 1.0 convolution_bitcast_fusion
  39.3 1.0 fusion.3
  40.4 1.1 fusion.2
  41.5 0.9 convolution_convert_fusion.2
  42.4 1.0 convolution_convert_fusion.1
  43.3 1.1 convolution_convert_fusion
  44.5 88.2 %all-reduce.4.cloned.1.call-done = (f32[256,256]{0,1:T(8,128)}, f32[512,256]{0,1:T(8,128)}) async-done(((f32[256,256]{0,1:T(8,128)}, f32[512,256]{0,1:T(8,128)}), (f32[256,256]{0,1:T(8,128)}, f32[512,256]{0,1:T(8,128)})) %all-reduce.4.cloned.1.call-update) | async-done | bytes 786448 | tf_op jit(solution)/shard_map/psum | solution.py:81
  132.6 1.8 copy.17
  134.4 2.0 copy.18
  136.4 63.2 %reduce-scatter.2.cloned.1.call-done = f32[160,256]{1,0:T(8,128)} async-done(((f32[2560,256]{1,0:T(8,128)}), f32[160,256]{1,0:T(8,128)}) %reduce-scatter.2.cloned.1.call-update) | async-done | bytes 163856 | tf_op jit(solution)/shard_map/reduce_scatter | solution.py:70
  199.7 6.2 %all-gather.1 = f32[320,256]{1,0:T(8,128)S(1)} all-gather(f32[160,256]{1,0:T(8,128)} %reduce-scatter.2.cloned.1.call-done), channel_id=3, replica_groups=mesh['dp'=16,'rows'=2] {'rows'}, dimensions={0}, use_global_device_ids=true | all-gather | bytes 491520 | tf_op jit(solution)/shard_map/all_gather | solution.py:71
  205.9 0.7 reduce_sum.29
  (33 shorter events, 3.8 us)
Async XLA Ops:
  7.2 13.4 %copy-start = (bf16[1,16,64,256]{3,2,1,0:T(8,128)(2,1)S(1)}, bf16[1,16,64,256]{3,2,1,0:T(8,128)(2,1)}, u32[]{:S(2)}) copy-start(bf16[1,16,64,256]{3,2,1,0:T(8,128)(2,1)} %param.9) | copy-start | bytes 1572868
  7.2 125.4 %all-reduce.4.cloned.1.call-start = ((), (), s32[]{:S(2)}) async-start(), calls=%async_computation.2 | async-start | bytes 1572864 | tf_op jit(solution)/shard_map/psum | solution.py:81
  8.1 6.5 %collective-permute-start = (bf16[1,1,64,256]{3,2,1,0:T(8,128)(2,1)S(1)}, bf16[1,1,64,256]{3,2,1,0:T(8,128)(2,1)S(1)}, u32[]{:S(2)}, u32[]{:S(2)}) collective-permute-start(bf16[1,1,64,256]{3,2,1,0:T(8,128)(2,1)S(1)} %get-tuple-element.28), channel_id=1, source_target_pairs={{0,1},{2,3},{4,5},{6,7},{8,9},{10,11},{12,13},{14,15},{16,17},{18,... | collective-permute-start | bytes 98312 | tf_op jit(solution)/shard_map/ppermute | solution.py:14
  13.0 5.8 %collective-permute-start.1 = (bf16[1,1,64,256]{3,2,1,0:T(8,128)(2,1)S(1)}, bf16[1,1,64,256]{3,2,1,0:T(8,128)(2,1)S(1)}, u32[]{:S(2)}, u32[]{:S(2)}) collective-permute-start(bf16[1,1,64,256]{3,2,1,0:T(8,128)(2,1)S(1)} %get-tuple-element.29), channel_id=1, source_target_pairs={{1,0},{3,2},{5,4},{7,6},{9,8},{11,10},{13,12},{15,14},{17,16},{19,... | collective-permute-start | bytes 98312 | tf_op jit(solution)/shard_map/ppermute | solution.py:15
  20.0 1.0 copy-start.1
  22.3 1.3 copy-start.3
  24.6 1.5 copy-start.2
  29.1 9.1 %copy-start.8 = (bf16[1,8,16,512]{3,2,1,0:T(8,128)(2,1)S(1)}, bf16[1,8,16,512]{3,2,1,0:T(8,128)(2,1)}, u32[]{:S(2)}) copy-start(bf16[1,8,16,512]{3,2,1,0:T(8,128)(2,1)} %param.13) | copy-start | bytes 393220
  35.7 4.7 %copy-start.4 = (bf16[1,16,64,256]{3,2,1,0:T(8,128)(2,1)S(1)}, bf16[1,16,64,256]{3,2,1,0:T(8,128)(2,1)}, u32[]{:S(2)}) copy-start(bf16[1,16,64,256]{3,2,1,0:T(8,128)(2,1)} %param.11) | copy-start | bytes 1572868
  39.3 2.2 %copy-start.5 = (bf16[512,256]{1,0:T(8,128)(2,1)S(1)}, bf16[512,256]{1,0:T(8,128)(2,1)}, u32[]{:S(2)}) copy-start(bf16[512,256]{1,0:T(8,128)(2,1)} %param.17) | copy-start | bytes 786436
  39.3 160.4 %reduce-scatter.2.cloned.1.call-start = ((), (), s32[]{:S(2)}) async-start(), calls=%async_computation.1 | async-start | bytes 2785280 | tf_op jit(solution)/shard_map/reduce_scatter | solution.py:70
  40.4 2.0 copy-start.6
  40.4 2.9 %copy-start.7 = (bf16[256,256]{1,0:T(8,128)(2,1)S(1)}, bf16[256,256]{1,0:T(8,128)(2,1)}, u32[]{:S(2)}) copy-start(bf16[256,256]{1,0:T(8,128)(2,1)} %param.15) | copy-start | bytes 393220
Sparse Core Ops, SparseCore 0:
  39.4 93.1 all-reduce.3
  136.4 63.2 reduce-scatter.1
